TPU v7x, 32 devices: a whole 2x2x4 slice. The times are simulated.
32 devices in a mesh: dist: 4 (over y, core), pix: 8 (over z, x).
Axes of the slice: x: 2, y: 2, z: 4, core: 2. Of those that a mesh axis runs over, the one named last changes fastest.
Arguments:
- contrast: float32 [4, 2, 2048, 2048], P('dist', None, 'pix'), may hold values from -6 to 6
- defocus: float32 [4], P('dist'), may hold values from 40 to 400
- blurring: float32 [4], P('dist'), may hold values from 0.5 to 4
Outputs:
- phase: float32 [2, 2048, 2048], P(None, 'pix')
All inputs are finite; a program needn't handle non-finite values.
Results may differ from a plain program's by a relative error of at most 0.0003.
Values sent between devices are 32-bit elements; how exact they have to be, the bound alone decides.
A program may use at most 64 MiB of HBM per device.

v0:
```python
import math

import jax
import jax.numpy as jnp
from jax import lax
from jax.sharding import PartitionSpec as P

ABSORB_RATIO = 0.1
REGULARIZER = 0.05


def unit_phase(first_len, second_len, period):
    left_index = jnp.arange(first_len, dtype=jnp.int32)[:, None]
    right_index = jnp.arange(second_len, dtype=jnp.int32)[None, :]
    turn_count = left_index * right_index % period
    angles = 2.0 * math.pi / period * turn_count.astype(jnp.float32)
    return (jnp.cos(angles), -jnp.sin(angles))


def conjugate_flip(tables):
    return (tables[0], -tables[1])


def complex_product(pattern, real_part, imag_part, tables):
    cosine, sine_part = tables
    out_real = jnp.einsum(pattern, real_part, cosine, precision=lax.Precision.HIGHEST) - jnp.einsum(
        pattern, imag_part, sine_part, precision=lax.Precision.HIGHEST
    )
    out_imag = jnp.einsum(
        pattern, real_part, sine_part, precision=lax.Precision.HIGHEST
    ) + jnp.einsum(pattern, imag_part, cosine, precision=lax.Precision.HIGHEST)
    return (out_real, out_imag)


def apply_twist(real_part, imag_part, cosine, sine_part):
    return (real_part * cosine - imag_part * sine_part, real_part * sine_part + imag_part * cosine)


def signed_square(freq_index, period):
    shifted = freq_index - period * (2 * freq_index >= period).astype(jnp.int32)
    fraction = shifted.astype(jnp.float32) / period
    return fraction * fraction


def transfer(defocus_value, blur_rate, squared):
    return jnp.exp(-blur_rate * squared) * (
        jnp.sin(defocus_value * squared) + ABSORB_RATIO * jnp.cos(defocus_value * squared)
    )


def body(contrast, defocus, blurring):
    images = contrast[0]
    projections, rows_local, columns = images.shape
    pix_count = lax.axis_size("pix")
    col_block = columns // pix_count
    rows_total = rows_local * pix_count
    outer_table = unit_phase(col_block, col_block, col_block)
    pixel_lookup_table = unit_phase(pix_count, pix_count, pix_count)
    row_table = unit_phase(rows_local, rows_local, rows_local)
    col_twist = unit_phase(col_block, pix_count, columns)
    row_twist = unit_phase(rows_local, pix_count, rows_total)
    even_images = images[0::2]
    odd_images = images[1::2]
    shaped_real = even_images.reshape(projections // 2, rows_local, col_block, pix_count)
    shaped_imag = odd_images.reshape(projections // 2, rows_local, col_block, pix_count)
    section_real, section_imag = complex_product(
        "prbn,bc->pcrn", shaped_real, shaped_imag, outer_table
    )
    section_real, section_imag = apply_twist(
        section_real, section_imag, col_twist[0][:, None, :], col_twist[1][:, None, :]
    )
    spec_real, spec_imag = complex_product(
        "pcrn,nq->pcrq", section_real, section_imag, pixel_lookup_table
    )
    col_freq = col_block * lax.axis_index("pix") + jnp.arange(col_block, dtype=jnp.int32)
    row_freq = (
        pix_count * jnp.arange(rows_local, dtype=jnp.int32)[:, None]
        + jnp.arange(pix_count, dtype=jnp.int32)[None, :]
    )
    squared = (
        signed_square(row_freq, rows_total)[None, :, :]
        + signed_square(col_freq, columns)[:, None, None]
    )
    own_gain = transfer(defocus[0], blurring[0], squared)
    received_real = lax.all_to_all(spec_real, "pix", split_axis=3, concat_axis=3, tiled=True)
    received_imaginary = lax.all_to_all(spec_imag, "pix", split_axis=3, concat_axis=3, tiled=True)
    middle_real, middle_imaginary = complex_product(
        "uhqb,bn->uhqn", received_real, received_imaginary, pixel_lookup_table
    )
    middle_real, middle_imaginary = apply_twist(
        middle_real, middle_imaginary, row_twist[0], row_twist[1]
    )
    out_real, out_imag = complex_product("pcrk,rj->pcjk", middle_real, middle_imaginary, row_table)
    summands = (own_gain * out_real, own_gain * out_imag, (own_gain * own_gain)[None])
    totals = lax.psum((summands[0], summands[1], summands[2]), "dist")
    den_sum = totals[2][0]
    bottom = 2.0 * (den_sum + REGULARIZER)
    quot_real = totals[0] / bottom
    quot_imag = totals[1] / bottom
    backward_real, backward_imaginary = complex_product(
        "pcjk,rj->pcrk", quot_real, quot_imag, conjugate_flip(row_table)
    )
    backward_real, backward_imaginary = apply_twist(
        backward_real, backward_imaginary, row_twist[0], -row_twist[1]
    )
    backward_real, backward_imaginary = complex_product(
        "uotv,zv->uotz", backward_real, backward_imaginary, conjugate_flip(pixel_lookup_table)
    )
    backward_real = backward_real / rows_total
    backward_imaginary = backward_imaginary / rows_total
    twist_cos = col_twist[0]
    twist_sin = col_twist[1]
    received_real = lax.all_to_all(backward_real, "pix", split_axis=3, concat_axis=3, tiled=True)
    received_imaginary = lax.all_to_all(
        backward_imaginary, "pix", split_axis=3, concat_axis=3, tiled=True
    )
    middle_real, middle_imaginary = complex_product(
        "pcrq,nq->pcrn", received_real, received_imaginary, conjugate_flip(pixel_lookup_table)
    )
    cols_real, cols_imag = apply_twist(
        middle_real, middle_imaginary, twist_cos[:, None, :], -twist_sin[:, None, :]
    )
    phase_blocks = jnp.einsum(
        "pcrn,cb->prbn", cols_real, outer_table[0], precision=lax.Precision.HIGHEST
    ) + jnp.einsum("pcrn,cb->prbn", cols_imag, outer_table[1], precision=lax.Precision.HIGHEST)
    odd_blocks = jnp.einsum(
        "pcrn,cb->prbn", cols_imag, outer_table[0], precision=lax.Precision.HIGHEST
    ) - jnp.einsum("pcrn,cb->prbn", cols_real, outer_table[1], precision=lax.Precision.HIGHEST)
    paired_blocks = jnp.stack([phase_blocks, odd_blocks], axis=1)
    return (paired_blocks / columns).reshape(projections, rows_local, columns)


def solution(mesh):
    return jax.shard_map(
        body,
        mesh=mesh,
        in_specs=(P("dist", None, "pix", None), P("dist"), P("dist")),
        out_specs=P(None, "pix", None),
        check_vma=False,
    )
```

profile of v0, /device:TPU:0, one launch (start us, length us, event | category | flops | bytes accessed | tf_op | source)
XLA Modules:
  0.0 490.3 jit_solution(7486254267559087429)
XLA Ops:
  6.5 0.1 fusion.161
  6.6 3.9 fusion.322
  10.5 1.8 copy.154
  12.3 1.9 copy.78
  14.3 4.2 fusion.102
  18.5 4.2 fusion.90
  22.7 2.9 copy.155
  25.6 2.1 copy.80
  27.8 0.0 copy-start
  27.8 5.4 %convolution_subtract_fusion = f32[256,256,8]{1,0,2:T(8,128)S(1)} fusion(f32[256,256,8]{1,0,2:T(8,128)} %fusion.102, f32[256,256,8]{1,0,2:T(8,128)S(1)} %copy.80), kind=kOutput, calls=%fused_computation.91 | convolution fusion | flops 1612120064 | bytes 6291456 | tf_op jit(solution)/shard_map/prbn,bc->pcrn/dot_general | solution.py:26
  33.2 5.2 %multiply_subtract_fusion.2 = (f32[256,256,8]{1,0,2:T(8,128)S(1)}, f32[256,256,8]{1,0,2:T(8,128)S(1)}) fusion(f32[256,256,8]{1,0,2:T(8,128)S(1)} %convolution_subtract_fusion, f32[256,8]{0,1:T(8,128)S(1)} %get-tuple-element.19, f32[256,8]{0,1:T(8,128)S(1)} %get-tuple-element.18, f32[256,256,8]{1,0,2:T(8,128)S(1)} %copy-done.4, f32[256,256,8]{1,0,2:T(8,128)} %copy-done), kind=kOutput, calls=%fused_computation.59 | convolution fusion | flops 1615200256 | bytes 10502144 | tf_op jit(solution)/shard_map/prbn,bc->pcrn/dot_general | solution.py:31
  38.4 3.2 fusion.50
  41.6 0.0 copy-done.1
  41.6 3.6 add_bitcast_fusion.1
  45.2 2.0 copy.94
  47.1 7.3 %all-to-all-start.1 = ((f32[1,256,256,8]{2,1,0,3:T(8,128)}), f32[1,256,256,8]{2,1,0,3:T(8,128)}, u32[]{:S(2)}, u32[]{:S(2)}) async-start(f32[1,256,256,8]{2,1,0,3:T(8,128)} %copy.94), calls=%async_computation.1 | async-start | bytes 4194304 | tf_op jit(solution)/shard_map/all_to_all | solution.py:86
  54.4 4.7 fusion.52
  59.1 3.2 subtract_bitcast_fusion.1
  62.3 2.0 copy.87
  64.3 38.4 %all-to-all-done.1 = f32[1,256,256,8]{2,1,0,3:T(8,128)} async-done(((f32[1,256,256,8]{2,1,0,3:T(8,128)}), f32[1,256,256,8]{2,1,0,3:T(8,128)}, u32[]{:S(2)}, u32[]{:S(2)}) %all-to-all-start.1) | async-done | bytes 2097184 | tf_op jit(solution)/shard_map/all_to_all | solution.py:86
  102.7 3.6 all-to-all-start
  106.4 0.0 all-reduce.3.cloned.1.call-start
  107.8 9.4 %fusion.80 = f32[1,256,256,8]{1,2,3,0:T(8,128)} fusion(f32[]{:T(128)} %bitcast.201, f32[256]{0:T(256)S(1)} %fusion.189, f32[256,8]{0,1:T(8,128)S(1)} %multiply_multiply_fusion, f32[]{:T(128)} %bitcast.2), kind=kLoop, calls=%fused_computation.92 | loop fusion | flops 3670016 | bytes 2106376 | tf_op jit(solution)/shard_map/mul | solution.py:94
  117.2 6.0 %fusion.28 = f32[256,256,8]{1,2,0:T(8,128)} fusion(f32[1,256,256,8]{2,1,0,3:T(8,128)} %all-to-all-done.1), kind=kOutput, calls=%fused_computation.37 | convolution fusion | flops 50332608 | bytes 4194304 | tf_op jit(solution)/shard_map/uhqb,bn->uhqn/dot_general | solution.py:26
  123.2 6.1 %fusion.26 = f32[256,256,8]{1,2,0:T(8,128)} fusion(f32[1,256,256,8]{2,1,0,3:T(8,128)} %all-to-all-done.1), kind=kOutput, calls=%fused_computation.35 | convolution fusion | flops 50332544 | bytes 4194304 | tf_op jit(solution)/shard_map/uhqb,bn->uhqn/dot_general | solution.py:31
  129.2 25.6 %all-to-all-done = f32[1,256,256,8]{2,1,0,3:T(8,128)S(1)} async-done(((f32[1,256,256,8]{2,1,0,3:T(8,128)}), f32[1,256,256,8]{2,1,0,3:T(8,128)S(1)}, u32[]{:S(2)}, u32[]{:S(2)}) %all-to-all-start) | async-done | bytes 2097184 | tf_op jit(solution)/shard_map/all_to_all | solution.py:85
  154.8 5.1 %fusion.68 = f32[256,256,8]{1,2,0:T(8,128)S(1)} fusion(f32[256,256,8]{1,2,0:T(8,128)} %fusion.28, f32[1,256,256,8]{2,1,0,3:T(8,128)S(1)} %all-to-all-done), kind=kOutput, calls=%fused_computation.86 | convolution fusion | flops 50856832 | bytes 6291456 | tf_op jit(solution)/shard_map/uhqb,bn->uhqn/dot_general | solution.py:26
  159.9 3.8 multiply_subtract_fusion.1
  163.8 3.3 fusion.40
  167.1 3.3 fusion.38
  170.3 13.1 %bitcast_multiply_fusion.1 = f32[1,256,256,8]{1,2,3,0:T(8,128)} fusion(f32[256,256,8]{1,0,2:T(8,128)S(1)} %fusion.40, f32[256,256,8]{1,2,0:T(8,128)S(1)} %get-tuple-element.12, f32[]{:T(128)} %bitcast.200, f32[256]{0:T(256)S(1)} %fusion.189, f32[256,8]{0,1:T(8,128)S(1)} %multiply_multiply_fusion, f32[]{:T(128)} %bitcast.2), kind=kOutput, calls=%fused_computation.10 | convolution fusion | flops 1615724544 | bytes 6300680 | tf_op jit(solution)/shard_map/pcrk,rj->pcjk/dot_general | solution.py:26
  183.4 12.9 %bitcast_multiply_fusion = f32[1,256,256,8]{1,2,3,0:T(8,128)} fusion(f32[256,256,8]{1,0,2:T(8,128)S(1)} %fusion.38, f32[256,256,8]{1,2,0:T(8,128)S(1)} %get-tuple-element.12, f32[]{:T(128)} %bitcast.202, f32[256]{0:T(256)S(1)} %fusion.189, f32[256,8]{0,1:T(8,128)S(1)} %multiply_multiply_fusion, f32[]{:T(128)} %bitcast.2), kind=kOutput, calls=%fused_computation.9 | convolution fusion | flops 1615790080 | bytes 6300680 | tf_op jit(solution)/shard_map/pcrk,rj->pcjk/dot_general | solution.py:29
  196.3 0.0 all-reduce.3.cloned.1.call-update
  196.3 0.1 fusion.160
  196.4 118.8 %all-reduce.3.cloned.1.call-done = (f32[1,256,256,8]{1,2,3,0:T(8,128)}, f32[1,256,256,8]{1,2,3,0:T(8,128)}, f32[1,256,256,8]{1,2,3,0:T(8,128)}) async-done(((f32[1,256,256,8]{1,2,3,0:T(8,128)}, f32[1,256,256,8]{1,2,3,0:T(8,128)}, f32[1,256,256,8]{1,2,3,0:T(8,128)}), (f32[1,256,256,8]{1,2,3,0:T(8,128)}, f32[1,256,256,8]{1,2,3,0:T(8,128)}, f32[1,256,256,8]{1,2,3,0:T(8,128)})) %all-reduce.3.cloned.1.call-update) | async-done | bytes 6291472 | tf_op jit(solution)/shard_map/psum | solution.py:95
  315.2 5.4 %fusion.18 = f32[256,256,8]{1,0,2:T(8,128)S(1)} fusion(f32[1,256,256,8]{1,2,3,0:T(8,128)} %get-tuple-element.5, f32[1,256,256,8]{1,2,3,0:T(8,128)} %get-tuple-element.6), kind=kOutput, calls=%fused_computation.27 | convolution fusion | flops 1613103104 | bytes 6291456 | tf_op jit(solution)/shard_map/pcjk,rj->pcrk/dot_general | solution.py:31
  320.7 3.3 fusion.20
  324.0 3.1 fusion.74
  327.2 5.7 %fusion.17 = (f32[256,256,8]{0,1,2:T(8,128)}, f32[256,256,8]{0,1,2:T(8,128)}) fusion(f32[256,256,8]{1,0,2:T(8,128)S(1)} %fusion.74, f32[256,8]{0,1:T(8,128)S(1)} %fusion.160, f32[256,8]{0,1:T(8,128)S(1)} %get-tuple-element.18, f32[256,256,8]{1,0,2:T(8,128)S(1)} %fusion.18, f32[1,256,256,8]{1,2,3,0:T(8,128)S(1)} %copy-done.8, ...), kind=kOutput, calls=%fused_computation.24 | convolution fusion | flops 1616773120 | bytes 12599296 | tf_op jit(solution)/shard_map/pcjk,rj->pcrk/dot_general | solution.py:29
  332.9 2.2 copy.111
  335.1 3.2 fusion.152
  338.3 2.6 copy.112
  340.9 3.6 multiply_bitcast_fusion.1
  344.5 2.0 copy.113
  346.5 5.5 %all-to-all-start.2 = ((f32[1,256,256,8]{2,1,0,3:T(8,128)}), f32[1,256,256,8]{2,1,0,3:T(8,128)}, u32[]{:S(2)}, u32[]{:S(2)}) async-start(f32[1,256,256,8]{2,1,0,3:T(8,128)} %copy.113), calls=%async_computation.2 | async-start | bytes 4194304 | tf_op jit(solution)/shard_map/all_to_all | solution.py:113
  352.0 3.5 fusion.142
  355.6 2.0 multiply_bitcast_fusion
  357.6 2.0 copy.117
  359.6 40.4 %all-to-all-done.2 = f32[1,256,256,8]{2,1,0,3:T(8,128)} async-done(((f32[1,256,256,8]{2,1,0,3:T(8,128)}), f32[1,256,256,8]{2,1,0,3:T(8,128)}, u32[]{:S(2)}, u32[]{:S(2)}) %all-to-all-start.2) | async-done | bytes 2097184 | tf_op jit(solution)/shard_map/all_to_all | solution.py:113
  400.0 3.8 all-to-all-start.3
  403.8 6.1 %fusion.10 = f32[256,256,8]{1,2,0:T(8,128)} fusion(f32[1,256,256,8]{2,1,0,3:T(8,128)} %all-to-all-done.2), kind=kOutput, calls=%fused_computation.15 | convolution fusion | flops 50332544 | bytes 4194304 | tf_op jit(solution)/shard_map/pcrq,nq->pcrn/dot_general | solution.py:29
  409.9 5.9 %fusion.12 = f32[256,256,8]{1,2,0:T(8,128)} fusion(f32[1,256,256,8]{2,1,0,3:T(8,128)} %all-to-all-done.2), kind=kOutput, calls=%fused_computation.17 | convolution fusion | flops 50332544 | bytes 4194304 | tf_op jit(solution)/shard_map/pcrq,nq->pcrn/dot_general | solution.py:26
  415.8 36.3 %all-to-all-done.3 = f32[1,256,256,8]{2,1,0,3:T(8,128)S(1)} async-done(((f32[1,256,256,8]{2,1,0,3:T(8,128)}), f32[1,256,256,8]{2,1,0,3:T(8,128)S(1)}, u32[]{:S(2)}, u32[]{:S(2)}) %all-to-all-start.3) | async-done | bytes 2097184 | tf_op jit(solution)/shard_map/all_to_all | solution.py:114
  452.1 3.0 fusion.6
  455.1 3.3 fusion.8
  458.5 2.7 multiply_subtract_fusion
  461.1 2.9 fusion.97
  464.0 2.9 fusion.95
  466.9 2.9 add_bitcast_fusion
  469.9 1.5 copy.241
  471.4 2.9 subtract_bitcast_fusion
  474.3 1.2 copy.240
  475.5 2.2 maximum_multiply_fusion
  477.7 5.3 %copy.125 = f32[2,256,2048]{2,1,0:T(8,128)} copy(f32[2,256,2048]{1,2,0:T(8,128)} %maximum_multiply_fusion) | data formatting | bytes 8388608 | tf_op jit(solution)/shard_map/div | solution.py:130
  (21 shorter events, 0.1 us)
Async XLA Ops:
  27.8 5.4 %copy-start = (f32[256,256,8]{1,0,2:T(8,128)}, f32[256,256,8]{1,0,2:T(8,128)S(1)}, u32[]{:S(2)}) copy-start(f32[256,256,8]{1,0,2:T(8,128)S(1)} %copy.80) | copy-start | bytes 6291460
  27.8 5.4 %copy-start.4 = (f32[256,256,8]{1,0,2:T(8,128)S(1)}, f32[256,256,8]{1,0,2:T(8,128)}, u32[]{:S(2)}) copy-start(f32[256,256,8]{1,0,2:T(8,128)} %fusion.90) | copy-start | bytes 6291460
  38.4 3.2 copy-start.1
  47.1 55.6 %all-to-all-start.1 = ((f32[1,256,256,8]{2,1,0,3:T(8,128)}), f32[1,256,256,8]{2,1,0,3:T(8,128)}, u32[]{:S(2)}, u32[]{:S(2)}) async-start(f32[1,256,256,8]{2,1,0,3:T(8,128)} %copy.94), calls=%async_computation.1 | async-start | bytes 4194304 | tf_op jit(solution)/shard_map/all_to_all | solution.py:86
  102.7 52.1 %all-to-all-start = ((f32[1,256,256,8]{2,1,0,3:T(8,128)}), f32[1,256,256,8]{2,1,0,3:T(8,128)S(1)}, u32[]{:S(2)}, u32[]{:S(2)}) async-start(f32[1,256,256,8]{2,1,0,3:T(8,128)} %copy.87), calls=%async_computation | async-start | bytes 4194304 | tf_op jit(solution)/shard_map/all_to_all | solution.py:85
  106.4 208.8 %all-reduce.3.cloned.1.call-start = ((), (), s32[]{:S(2)}) async-start(), calls=%async_computation.4 | async-start | bytes 12582912 | tf_op jit(solution)/shard_map/psum | solution.py:95
  154.8 5.1 %copy-start.3 = (f32[256,256,8]{1,2,0:T(8,128)S(1)}, f32[256,256,8]{1,2,0:T(8,128)}, u32[]{:S(2)}) copy-start(f32[256,256,8]{1,2,0:T(8,128)} %fusion.26) | copy-start | bytes 6291460
  315.2 5.5 %copy-start.7 = (f32[1,256,256,8]{1,2,3,0:T(8,128)S(1)}, f32[1,256,256,8]{1,2,3,0:T(8,128)}, u32[]{:S(2)}) copy-start(f32[1,256,256,8]{1,2,3,0:T(8,128)} %get-tuple-element.6) | copy-start | bytes 6291460
  315.2 5.5 %copy-start.9 = (f32[1,256,256,8]{1,2,3,0:T(8,128)S(1)}, f32[1,256,256,8]{1,2,3,0:T(8,128)}, u32[]{:S(2)}) copy-start(f32[1,256,256,8]{1,2,3,0:T(8,128)} %get-tuple-element.5) | copy-start | bytes 6291460
  320.7 3.3 copy-start.8
  335.1 3.2 copy-start.2
  346.5 53.5 %all-to-all-start.2 = ((f32[1,256,256,8]{2,1,0,3:T(8,128)}), f32[1,256,256,8]{2,1,0,3:T(8,128)}, u32[]{:S(2)}, u32[]{:S(2)}) async-start(f32[1,256,256,8]{2,1,0,3:T(8,128)} %copy.113), calls=%async_computation.2 | async-start | bytes 4194304 | tf_op jit(solution)/shard_map/all_to_all | solution.py:113
  400.0 52.1 %all-to-all-start.3 = ((f32[1,256,256,8]{2,1,0,3:T(8,128)}), f32[1,256,256,8]{2,1,0,3:T(8,128)S(1)}, u32[]{:S(2)}, u32[]{:S(2)}) async-start(f32[1,256,256,8]{2,1,0,3:T(8,128)} %copy.117), calls=%async_computation.3 | async-start | bytes 4194304 | tf_op jit(solution)/shard_map/all_to_all | solution.py:114
  455.1 3.3 copy-start.5
  455.1 3.3 copy-start.6
Sparse Core Ops, SparseCore 0:
  196.4 118.6 all-reduce.2
where the time goes:
time: 497 us; the launch traced here: 490 us
  waiting for transfers between devices  260 us (52%)
  matrix products  147 us (30%)
  local copies, waits for them, and re-layouts  33.6 us (7%)
  starting transfers between devices  20.2 us (4%)
  between operations  15.5 us (3%)
  other arithmetic  14.5 us (3%)
    psum x1, waiting for transfers between devices, body(): totals = lax.psum((summands[0], summands[1], summands[2]), 'dist')  119 us
    all_to_all x1, waiting for transfers between devices, body(): lax.all_to_all(backward_real, 'pix', split_axis=3, concat_axis=3, tiled=T...  40.4 us
    dot_general x7, matrix products, complex_product(): jnp.einsum(pattern, real_part, sine_part, precision=lax.Precision.HIGHEST)  39.8 us
    all_to_all x1, waiting for transfers between devices, body(): lax.all_to_all(spec_imag, 'pix', split_axis=3, concat_axis=3, tiled=True)  38.4 us
    dot_general x7, matrix products, complex_product(): jnp.einsum(pattern, real_part, cosine, precision=lax.Precision.HIGHEST)  37.9 us
    all_to_all x1, waiting for transfers between devices, body(): lax.all_to_all(backward_imaginary, 'pix', split_axis=3, concat_axis=3, ti...  36.3 us
    dot_general x7, matrix products, complex_product(): jnp.einsum(pattern, imag_part, sine_part, precision=lax.Precision.HIGHEST)  29.5 us
    dot_general x7, matrix products, complex_product(): jnp.einsum(pattern, imag_part, cosine, precision=lax.Precision.HIGHEST)  28.2 us
  transfers between devices with their start and end apart: 5, of which 5 were waited for; matrix products, arithmetic and copies ran while one was open for 10% of the time, Pallas kernels for 0%

commit v1 on v0

--- a/solution.py
+++ b/solution.py
@@ -1,8 +1,12 @@
+import functools
 import math
 
 import jax
 import jax.numpy as jnp
+import numpy as np
 from jax import lax
+from jax.experimental import pallas as pl
+from jax.experimental.pallas import tpu as pltpu
 from jax.sharding import PartitionSpec as P
 
 ABSORB_RATIO = 0.1
@@ -48,7 +52,7 @@
     )
 
 
-def body(contrast, defocus, blurring):
+def general_body(contrast, defocus, blurring):
     images = contrast[0]
     projections, rows_local, columns = images.shape
     pix_count = lax.axis_size("pix")
@@ -130,6 +134,421 @@
     return (paired_blocks / columns).reshape(projections, rows_local, columns)
 
 
+RADIX = 8
+CHUNK = 16
+
+
+def split_bf16(value):
+    high = value.astype(jnp.bfloat16)
+    return high, (value - high.astype(jnp.float32)).astype(jnp.bfloat16)
+
+
+def split_table(table):
+    high = table.astype(np.float32).astype(jnp.bfloat16)
+    return high, (table - high.astype(np.float64)).astype(np.float32).astype(jnp.bfloat16)
+
+
+def dot_nt(left, right):
+    return lax.dot_general(left, right, (((1,), (1,)), ((), ())), preferred_element_type=jnp.float32)
+
+
+def dot_nn(left, right):
+    return lax.dot_general(left, right, (((1,), (0,)), ((), ())), preferred_element_type=jnp.float32)
+
+
+def dot3(dot, left, right):
+    return dot(left[0], right[0]) + (dot(left[0], right[1]) + dot(left[1], right[0]))
+
+
+def small_dft(items, sign, turn, add, sub):
+    count = len(items)
+    if count == 1:
+        return items
+    even = small_dft(items[0::2], sign, turn, add, sub)
+    odd = small_dft(items[1::2], sign, turn, add, sub)
+    low, high = [], []
+    for k in range(count // 2):
+        moved = odd[k]
+        if k:
+            moved = turn(moved, k, count, sign)
+        low.append(add(even[k], moved))
+        high.append(sub(even[k], moved))
+    return low + high
+
+
+def pair_turn(item, k, count, sign):
+    real, imag = item
+    if 4 * k == count:
+        return (-imag, real) if sign > 0 else (imag, -real)
+    angle = sign * 2.0 * math.pi * k / count
+    cosine, sine = math.cos(angle), math.sin(angle)
+    return (real * cosine - imag * sine, real * sine + imag * cosine)
+
+
+def pair_add(a, b):
+    return (a[0] + b[0], a[1] + b[1])
+
+
+def pair_sub(a, b):
+    return (a[0] - b[0], a[1] - b[1])
+
+
+pair_dft = functools.partial(small_dft, turn=pair_turn, add=pair_add, sub=pair_sub)
+
+
+def col_forward_kernel(x_ref, th_ref, tl_ref, tw_ref, out_ref, yh_ref, yl_ref):
+    _, rows, columns = x_ref.shape
+    block = columns // RADIX
+    per_q, _, width, _ = out_ref.shape[1:]
+
+    def spread(i, carry):
+        at = pl.ds(pl.multiple_of(i * CHUNK, CHUNK), CHUNK)
+        parts = [
+            (x_ref[0, at, j * block : (j + 1) * block], x_ref[1, at, j * block : (j + 1) * block])
+            for j in range(RADIX)
+        ]
+        for q, (real, imag) in enumerate(pair_dft(parts, -1)):
+            if q:
+                cosine, sine = tw_ref[q, 0:1, :], tw_ref[q, 1:2, :]
+                real, imag = real * cosine + imag * sine, imag * cosine - real * sine
+            for half, value in enumerate((real, imag)):
+                high, low = split_bf16(value)
+                yh_ref[q, at, half * block : (half + 1) * block] = high
+                yl_ref[q, at, half * block : (half + 1) * block] = low
+        return carry
+
+    lax.fori_loop(0, rows // CHUNK, spread, 0)
+
+    def transform(q, carry):
+        table = (th_ref[...], tl_ref[...])
+        result = dot3(dot_nt, table, (yh_ref[q], yl_ref[q]))
+        for part in range(per_q):
+            for half in range(2):
+                first = half * block + part * width
+                out_ref[q, part, half] = result[first : first + width]
+        return carry
+
+    lax.fori_loop(0, RADIX, transform, 0)
+
+
+def middle_kernel(scale, in_ref, th_ref, tl_ref, tw_ref, twc_ref, f_ref, g_ref, out_ref, yh_ref, yl_ref, t_ref):
+    dists, pixes, _, width, block = in_ref.shape
+    per_dist = width // CHUNK
+
+    def spread(i, carry):
+        dist = i // per_dist
+        at = pl.ds(pl.multiple_of((i % per_dist) * CHUNK, CHUNK), CHUNK)
+        to = pl.ds(pl.multiple_of(i * CHUNK, CHUNK), CHUNK)
+        parts = [(in_ref[dist, j, 0, at, :], in_ref[dist, j, 1, at, :]) for j in range(pixes)]
+        for q, (real, imag) in enumerate(pair_dft(parts, -1)):
+            if q:
+                cosine, sine = tw_ref[q, 0:1, :], tw_ref[q, 1:2, :]
+                real, imag = real * cosine + imag * sine, imag * cosine - real * sine
+            for half, value in enumerate((real, imag)):
+                high, low = split_bf16(value)
+                yh_ref[q, to, half * block : (half + 1) * block] = high
+                yl_ref[q, to, half * block : (half + 1) * block] = low
+        return carry
+
+    lax.fori_loop(0, dists * per_dist, spread, 0)
+
+    def transform(q, carry):
+        table = (th_ref[...], tl_ref[...])
+        spectrum = dot3(dot_nt, (yh_ref[q], yl_ref[q]), table)
+        factors = f_ref[q]
+        total_real = total_imag = bottom = None
+        for dist in range(dists):
+            gain = (
+                factors[2 * dist : 2 * dist + 1] * g_ref[2 * dist]
+                + factors[2 * dist + 1 : 2 * dist + 2] * g_ref[2 * dist + 1]
+            )
+            real = gain * spectrum[dist * width : (dist + 1) * width, :block]
+            imag = gain * spectrum[dist * width : (dist + 1) * width, block:]
+            square = gain * gain
+            if dist == 0:
+                total_real, total_imag, bottom = real, imag, square
+            else:
+                total_real, total_imag, bottom = total_real + real, total_imag + imag, bottom + square
+        ratio = scale / (2.0 * (bottom + REGULARIZER))
+        real, imag = total_real * ratio, total_imag * ratio
+        stacked = jnp.concatenate(
+            [jnp.concatenate([real, -imag], axis=1), jnp.concatenate([imag, real], axis=1)], axis=0
+        )
+        upper = (th_ref[:block, :], tl_ref[:block, :])
+        t_ref[q] = dot3(dot_nt, upper, split_bf16(stacked))
+        return carry
+
+    lax.fori_loop(0, RADIX, transform, 0)
+
+    lane = lax.broadcasted_iota(jnp.int32, (CHUNK, 2 * width), 1)
+    flip = jnp.where(lane < width, -1.0, 1.0).astype(jnp.float32)
+
+    def times_i(value):
+        return pltpu.roll(value, width, 1) * flip
+
+    def turn(value, k, count, sign):
+        if 4 * k == count:
+            return times_i(value)
+        angle = sign * 2.0 * math.pi * k / count
+        return value * math.cos(angle) + times_i(value) * math.sin(angle)
+
+    def gather(i, carry):
+        at = pl.ds(pl.multiple_of(i * CHUNK, CHUNK), CHUNK)
+        twists = twc_ref[at, :]
+        parts = []
+        for q in range(RADIX):
+            value = t_ref[q, at, :]
+            if q:
+                value = value * twists[:, q : q + 1] + times_i(value) * twists[:, RADIX + q : RADIX + q + 1]
+            parts.append(value)
+        done = small_dft(parts, 1, turn, lambda a, b: a + b, lambda a, b: a - b)
+        for j in range(pixes):
+            out_ref[j, at, :] = done[j]
+        return carry
+
+    lax.fori_loop(0, block // CHUNK, gather, 0)
+
+
+def col_inverse_kernel(in_ref, th_ref, tl_ref, tw_ref, out_ref, ah_ref, al_ref, t_ref):
+    _, per_q, rows, lanes = in_ref.shape
+    block = per_q * lanes // 2
+    for q in range(RADIX):
+        for part in range(per_q):
+            high, low = split_bf16(in_ref[q, part])
+            ah_ref[q * rows : (q + 1) * rows, part * lanes : (part + 1) * lanes] = high
+            al_ref[q * rows : (q + 1) * rows, part * lanes : (part + 1) * lanes] = low
+    t_ref[...] = dot3(dot_nn, (ah_ref[...], al_ref[...]), (th_ref[...], tl_ref[...]))
+
+    def gather(i, carry):
+        at = pl.ds(pl.multiple_of(i * CHUNK, CHUNK), CHUNK)
+        parts = []
+        for q in range(RADIX):
+            row = pl.ds(pl.multiple_of(q * rows + i * CHUNK, CHUNK), CHUNK)
+            real, imag = t_ref[row, :block], t_ref[row, block:]
+            if q:
+                cosine, sine = tw_ref[q, 0:1, :], tw_ref[q, 1:2, :]
+                real, imag = real * cosine - imag * sine, imag * cosine + real * sine
+            parts.append((real, imag))
+        for j, (real, imag) in enumerate(pair_dft(parts, 1)):
+            out_ref[0, at, j * block : (j + 1) * block] = real
+            out_ref[1, at, j * block : (j + 1) * block] = imag
+        return carry
+
+    lax.fori_loop(0, rows // CHUNK, gather, 0)
+
+
+def exchange_kernel(dists, pixes, in_ref, out_ref, send_sem, recv_sem, own_sem):
+    dist, pix = lax.axis_index("dist"), lax.axis_index("pix")
+    count = dists * pixes
+    me = dist * pixes + pix
+    own = pltpu.make_async_copy(in_ref.at[me], out_ref.at[me], own_sem)
+    own.start()
+
+    def copy(step):
+        target = (me + step) % count
+        return pltpu.make_async_remote_copy(
+            src_ref=in_ref.at[target],
+            dst_ref=out_ref.at[me],
+            send_sem=send_sem.at[step],
+            recv_sem=recv_sem.at[step],
+            device_id={"dist": target // pixes, "pix": target % pixes},
+            device_id_type=pl.DeviceIdType.MESH,
+        )
+
+    def start(step, carry):
+        copy(step).start()
+        return carry
+
+    def finish(step, carry):
+        copy(step).wait_send()
+        source = (me + count - step) % count
+        pltpu.make_async_remote_copy(
+            src_ref=in_ref.at[source],
+            dst_ref=out_ref.at[source],
+            send_sem=send_sem.at[step],
+            recv_sem=recv_sem.at[step],
+            device_id={"dist": source // pixes, "pix": source % pixes},
+            device_id_type=pl.DeviceIdType.MESH,
+        ).wait_recv()
+        return carry
+
+    lax.fori_loop(1, count, start, 0)
+    lax.fori_loop(1, count, finish, 0)
+    own.wait()
+
+
+def exchange(dists, pixes, array):
+    count = dists * pixes
+    return pl.pallas_call(
+        functools.partial(exchange_kernel, dists, pixes),
+        out_shape=jax.ShapeDtypeStruct(array.shape, array.dtype),
+        in_specs=[pl.BlockSpec(memory_space=pl.ANY)],
+        out_specs=pl.BlockSpec(memory_space=pl.ANY),
+        scratch_shapes=[
+            pltpu.SemaphoreType.DMA((count,)),
+            pltpu.SemaphoreType.DMA((count,)),
+            pltpu.SemaphoreType.DMA,
+        ],
+        compiler_params=pltpu.CompilerParams(has_side_effects=True),
+    )(array)
+
+
+GATHER_PIECES = 4
+
+
+def gather_kernel(in_ref, out_ref, sems, own_sem):
+    dist = lax.axis_index("dist")
+    rows = in_ref.shape[1]
+    piece = rows // GATHER_PIECES
+    mate = dist + 1 - 2 * (dist % 2)
+    across = (dist + 2) % 4
+    corner = (mate + 2) % 4
+
+    def at(owner, c):
+        return out_ref.at[:, pl.ds(pl.multiple_of(owner * rows + c * piece, piece), piece), :]
+
+    def send(src, owner, c, kind, target):
+        return pltpu.make_async_remote_copy(
+            src_ref=src,
+            dst_ref=at(owner, c),
+            send_sem=sems.at[0, kind, c],
+            recv_sem=sems.at[1, kind, c],
+            device_id={"dist": target},
+            device_id_type=pl.DeviceIdType.MESH,
+        )
+
+    def local(c):
+        return in_ref.at[:, pl.ds(c * piece, piece), :]
+
+    own = pltpu.make_async_copy(in_ref, out_ref.at[:, pl.ds(pl.multiple_of(dist * rows, rows), rows), :], own_sem)
+    for c in range(GATHER_PIECES):
+        send(local(c), dist, c, 0, across).start()
+    for c in range(GATHER_PIECES):
+        send(local(c), dist, c, 1, mate).start()
+    own.start()
+    for c in range(GATHER_PIECES):
+        send(local(c), across, c, 0, across).wait_recv()
+        send(at(across, c), across, c, 2, mate).start()
+    for c in range(GATHER_PIECES):
+        send(local(c), dist, c, 0, across).wait_send()
+        send(local(c), mate, c, 1, mate).wait()
+        send(at(across, c), across, c, 2, mate).wait_send()
+        send(at(across, c), corner, c, 2, mate).wait_recv()
+    own.wait()
+
+
+def gather_dist(dists, array):
+    pair, rows, columns = array.shape
+    return pl.pallas_call(
+        gather_kernel,
+        out_shape=jax.ShapeDtypeStruct((pair, dists * rows, columns), array.dtype),
+        in_specs=[pl.BlockSpec(memory_space=pl.ANY)],
+        out_specs=pl.BlockSpec(memory_space=pl.ANY),
+        scratch_shapes=[pltpu.SemaphoreType.DMA((2, 3, GATHER_PIECES)), pltpu.SemaphoreType.DMA],
+        compiler_params=pltpu.CompilerParams(has_side_effects=True),
+    )(array)
+
+
+def freq_square(order, period):
+    freq = RADIX * (order % (period // RADIX)) + order // (period // RADIX)
+    return signed_square(freq, period)
+
+
+def gain_factors(defocus, blurring, squared):
+    envelope = jnp.exp(-blurring[:, None] * squared)
+    sine = envelope * jnp.sin(defocus[:, None] * squared)
+    cosine = envelope * jnp.cos(defocus[:, None] * squared)
+    return sine, cosine
+
+
+def vmem_call(kernel, out_shape, scratch, *args):
+    return pl.pallas_call(
+        kernel,
+        out_shape=jax.ShapeDtypeStruct(out_shape, jnp.float32),
+        in_specs=[pl.BlockSpec(memory_space=pltpu.VMEM)] * len(args),
+        out_specs=pl.BlockSpec(memory_space=pltpu.VMEM),
+        scratch_shapes=scratch,
+    )(*args)
+
+
+def fast_body(contrast, defocus, blurring):
+    images = contrast[0]
+    _, rows, columns = images.shape
+    pixes, dists = lax.axis_size("pix"), lax.axis_size("dist")
+    count = pixes * dists
+    block = columns // RADIX
+    width = columns // count
+    per_q = block // width
+    total_rows = rows * pixes
+    out_rows = rows // dists
+
+    turns = np.outer(np.arange(block), np.arange(block)) % block * (2.0 * np.pi / block)
+    cosine, sine = np.cos(turns), np.sin(turns)
+    table = np.block([[cosine, sine], [-sine, cosine]])
+    order = np.concatenate(
+        [np.arange(width) + part * width + half * block for part in range(per_q) for half in range(2)]
+    )
+    th, tl = split_table(table)
+    ph, pl_ = split_table(table[order])
+    twist = np.outer(np.arange(RADIX), np.arange(block)) * (2.0 * np.pi / columns)
+    tw = np.stack([np.cos(twist), np.sin(twist)], axis=1).astype(np.float32)
+    twc = np.concatenate([np.cos(twist).T, np.sin(twist).T], axis=1).astype(np.float32)
+
+    both = lax.all_gather(jnp.concatenate([defocus, blurring]), "dist")
+    defocus_all, blurring_all = both[:, 0], both[:, 1]
+    row_sine, row_cosine = gain_factors(
+        defocus_all, blurring_all, freq_square(jnp.arange(total_rows, dtype=jnp.int32), total_rows)[None]
+    )
+    me = lax.axis_index("dist") * pixes + lax.axis_index("pix")
+    col_sine, col_cosine = gain_factors(
+        defocus_all, blurring_all, freq_square(me * width + jnp.arange(width, dtype=jnp.int32), columns)[None]
+    )
+    f_table = jnp.stack([row_sine, row_cosine], axis=1).reshape(2 * dists, RADIX, rows).transpose(1, 0, 2)
+    g_table = jnp.stack(
+        [col_cosine - ABSORB_RATIO * col_sine, col_sine + ABSORB_RATIO * col_cosine], axis=1
+    ).reshape(2 * dists, width, 1)
+    g_table = jnp.broadcast_to(g_table, (2 * dists, width, rows))
+
+    spectra = vmem_call(
+        col_forward_kernel,
+        (RADIX, per_q, 2, width, rows),
+        [pltpu.VMEM((RADIX, rows, 2 * block), jnp.bfloat16)] * 2,
+        images, th, tl, tw,
+    )
+    received = exchange(dists, pixes, spectra.reshape(count, 2, width, rows))
+    back = vmem_call(
+        functools.partial(middle_kernel, 1.0 / (total_rows * columns)),
+        (pixes, rows, 2 * width),
+        [pltpu.VMEM((RADIX, dists * width, 2 * rows), jnp.bfloat16)] * 2
+        + [pltpu.VMEM((RADIX, rows, 2 * width), jnp.float32)],
+        received.reshape(dists, pixes, 2, width, rows), th, tl, tw, twc, f_table, g_table,
+    )
+    back = back.reshape(pixes, dists, out_rows, 2 * width).transpose(1, 0, 2, 3)
+    arrived = exchange(dists, pixes, back.reshape(count, out_rows, 2 * width))
+    phase = vmem_call(
+        col_inverse_kernel,
+        (2, out_rows, columns),
+        [pltpu.VMEM((RADIX * out_rows, 2 * block), jnp.bfloat16)] * 2
+        + [pltpu.VMEM((RADIX * out_rows, 2 * block), jnp.float32)],
+        arrived.reshape(RADIX, per_q, out_rows, 2 * width), ph, pl_, tw,
+    )
+    return gather_dist(dists, phase)
+
+
+def body(contrast, defocus, blurring):
+    _, projections, rows, columns = contrast.shape
+    pixes, dists = lax.axis_size("pix"), lax.axis_size("dist")
+    fits = (
+        projections == 2
+        and pixes == RADIX
+        and dists == 4
+        and rows * pixes == columns
+        and columns % (dists * pixes * 64) == 0
+        and columns // (dists * pixes) == rows // dists == 64
+    )
+    return (fast_body if fits else general_body)(contrast, defocus, blurring)
+
+
 def solution(mesh):
     return jax.shard_map(
         body,

time: 497 us -> 226 us (0.45); the launches traced: 490 us -> 226 us
  waiting for transfers between devices: 260 us -> 0 us
  Pallas kernels: 0 us -> 208 us
  matrix products: 147 us -> 0 us
  local copies, waits for them, and re-layouts: 33.6 us -> 9.38 us
  starting transfers between devices: 20.2 us -> 0 us
  other arithmetic: 14.5 us -> 0.85 us
  between operations: 15.5 us -> 2.04 us
  blocking collectives: 0 us -> 5.83 us
    pallas_call x0 -> x6, Pallas kernels: none -> 208 us  [the longest x2 137 us: exchange(): pl.pallas_call(functools.partial(exchange_kernel, dists, pixes), out_shap...]
    dot_general x32 -> x0, matrix products: 147 us -> none  [the longest x7 39.8 us: complex_product(): jnp.einsum(pattern, real_part, sine_part, precision=lax.Precision.HIGHEST)]
    all_to_all x4 -> x0, waiting for transfers between devices: 141 us -> none  [the longest x1 40.4 us: body(): lax.all_to_all(backward_real, 'pix', split_axis=3, concat_axis=3, tiled=T...]
    psum x1 -> x0, waiting for transfers between devices: 119 us -> none  [body(): totals = lax.psum((summands[0], summands[1], summands[2]), 'dist')]
    all_to_all x4 -> x0, starting transfers between devices: 20.2 us -> none  [the longest x1 7.28 us: body(): lax.all_to_all(spec_imag, 'pix', split_axis=3, concat_axis=3, tiled=True)]
    div x3 -> x0, local copies, waits for them, and re-layouts: 9.31 us -> none  [the longest x1 5.34 us: body(): return (paired_blocks / columns).reshape(projections, rows_local, columns)]
    mul x2 -> x1, other arithmetic: 9.42 us -> 0.32 us  [gain_factors(): sine = envelope * jnp.sin(defocus[:, None] * squared)]
    another operation x3 -> x2, local copies, waits for them, and re-layouts: 6.95 us -> 0.06 us  [the longest x1 0.05 us: fast_body(): jnp.stack([row_sine, row_cosine], axis=1).reshape(2 * dists, RADIX, rows)]
  transfers between devices with their start and end apart: 5 -> 0, of which waited for: 5 -> 0; matrix products, arithmetic and copies ran while one was open for 10% -> 0% of each run, Pallas kernels for 0% -> 0%
where the time goes in v1:
time: 226 us
  Pallas kernels  208 us (92%)
  local copies, waits for them, and re-layouts  9.38 us (4%)
  blocking collectives  5.83 us (3%)
    pallas_call x2, Pallas kernels, exchange(): pl.pallas_call(functools.partial(exchange_kernel, dists, pixes), out_shap...  137 us
    pallas_call x1, Pallas kernels, gather_dist(): pl.pallas_call(gather_kernel, out_shape=jax.ShapeDtypeStruct((pair, dists...  37 us
    pallas_call x3, Pallas kernels, vmem_call(): pl.pallas_call(kernel, out_shape=jax.ShapeDtypeStruct(out_shape, jnp.floa...  34.2 us
    unnamed x1, blocking collectives  5.83 us
    unnamed x5, local copies, waits for them, and re-layouts  5.29 us

profile of v1, /device:TPU:0, one launch (start us, length us, event | category | flops | bytes accessed | tf_op | source)
XLA Modules:
  0.0 226.0 jit_solution(17583853456576335759)
XLA Ops:
  0.0 10.9 %shard_map.91 = f32[8,4,2,64,256]{4,3,2,1,0:T(8,128)} custom-call(f32[2,256,2048]{2,1,0:T(8,128)} %bitcast.16, bf16[512,512]{1,0:T(8,128)(2,1)} %constant.88.clone.th_ref, bf16[512,512]{1,0:T(8,128)(2,1)} %constant.89.clone.tl_ref, f32[8,2,256]{2,1,0:T(2,128)} %constant.90.clone.tw_ref), custom_call_target="tpu_custom_call" | custom-call | tf_op jit(solution)/shard_map/pallas_call | solution.py:465
  10.9 0.0 copy-start
  10.9 99.2 %shard_map.92 = f32[32,2,64,256]{3,2,1,0:T(8,128)} custom-call(f32[32,2,64,256]{3,2,1,0:T(8,128)} %bitcast.14), custom_call_target="tpu_custom_call" | custom-call | tf_op jit(solution)/shard_map/pallas_call | solution.py:382
  110.1 0.0 copy-done
  110.1 0.6 dynamic-slice
  112.7 0.2 maximum_dynamic-update-slice_fusion
  112.8 5.8 %all-reduce = f32[8]{0:T(128)S(1)} all-reduce(f32[8]{0:T(128)S(1)} %maximum_dynamic-update-slice_fusion), channel_id=2, replica_groups=mesh['dist'=4,'pix'=8] {'dist'}, use_global_device_ids=true, to_apply=%add | all-reduce | flops 8 | bytes 64
  118.7 0.1 reshape.484
  118.8 0.2 negate_reduce_fusion
  119.0 0.3 fusion
  119.3 0.1 copy.16
  119.4 0.1 reshape.480
  119.4 0.6 copy.21
  120.1 0.1 multiply_subtract_fusion
  120.2 0.9 broadcast_in_dim.10.g_ref
  121.2 19.6 %shard_map.93 = f32[8,256,128]{2,1,0:T(8,128)} custom-call(f32[4,8,2,64,256]{4,3,2,1,0:T(8,128)} %bitcast.13, bf16[512,512]{1,0:T(8,128)(2,1)} %constant.88.clone.th_ref, bf16[512,512]{1,0:T(8,128)(2,1)} %constant.89.clone.tl_ref, f32[8,2,256]{2,1,0:T(2,128)} %constant.90.clone.tw_ref, f32[256,16]{1,0:T(8,128)} %constant.91.clone.twc_ref, ...), custom_call_target="tpu_custom_call" | custom-call | tf_op jit(solution)/shard_map/pallas_call | solution.py:465
  140.7 2.3 %copy.19 = f32[8,4,64,128]{3,2,0,1:T(8,128)} copy(f32[8,4,64,128]{3,2,1,0:T(8,128)} %bitcast.18) | data formatting | bytes 2097152 | tf_op jit(solution)/shard_map/reshape | solution.py:526
  143.1 37.5 %shard_map.94 = f32[32,64,128]{2,1,0:T(8,128)} custom-call(f32[32,64,128]{2,1,0:T(8,128)} %bitcast.17), custom_call_target="tpu_custom_call" | custom-call | tf_op jit(solution)/shard_map/pallas_call | solution.py:382
  180.6 3.8 %shard_map.95.in_ref = f32[2,64,2048]{2,1,0:T(8,128)} custom-call(f32[8,4,64,128]{3,2,1,0:T(8,128)} %bitcast.15, bf16[512,512]{1,0:T(8,128)(2,1)} %constant.92.clone.th_ref, bf16[512,512]{1,0:T(8,128)(2,1)} %constant.93.clone.tl_ref, f32[8,2,256]{2,1,0:T(2,128)} %constant.90.clone.tw_ref), custom_call_target="tpu_custom_call" | custom-call | tf_op jit(solution)/shard_map/pallas_call | solution.py:465
  184.3 37.0 %shard_map.96 = f32[2,256,2048]{2,1,0:T(8,128)} custom-call(f32[2,64,2048]{2,1,0:T(8,128)} %shard_map.95.in_ref), custom_call_target="tpu_custom_call" | custom-call | tf_op jit(solution)/shard_map/pallas_call | solution.py:442
  221.3 4.7 %copy.26 = f32[2,256,2048]{2,1,0:T(8,128)} copy(f32[2,256,2048]{2,1,0:T(8,128)} %shard_map.96) | data formatting | bytes 8388608
  (6 shorter events, 0.1 us)
Async XLA Ops:
  10.9 99.2 %copy-start = (u32[32]{0:T(128)S(1)}, u32[32]{0:T(128)}, u32[]{:S(2)}) copy-start(u32[32]{0:T(128)} %constant.99) | copy-start | bytes 388

commit v2 on v1

--- a/solution.py
+++ b/solution.py
@@ -312,19 +312,22 @@
 def col_inverse_kernel(in_ref, th_ref, tl_ref, tw_ref, out_ref, ah_ref, al_ref, t_ref):
     _, per_q, rows, lanes = in_ref.shape
     block = per_q * lanes // 2
-    for q in range(RADIX):
+
+    def transform(q, carry):
         for part in range(per_q):
             high, low = split_bf16(in_ref[q, part])
-            ah_ref[q * rows : (q + 1) * rows, part * lanes : (part + 1) * lanes] = high
-            al_ref[q * rows : (q + 1) * rows, part * lanes : (part + 1) * lanes] = low
-    t_ref[...] = dot3(dot_nn, (ah_ref[...], al_ref[...]), (th_ref[...], tl_ref[...]))
+            ah_ref[:, part * lanes : (part + 1) * lanes] = high
+            al_ref[:, part * lanes : (part + 1) * lanes] = low
+        t_ref[q] = dot3(dot_nn, (ah_ref[...], al_ref[...]), (th_ref[...], tl_ref[...]))
+        return carry
+
+    lax.fori_loop(0, RADIX, transform, 0)
 
     def gather(i, carry):
         at = pl.ds(pl.multiple_of(i * CHUNK, CHUNK), CHUNK)
         parts = []
         for q in range(RADIX):
-            row = pl.ds(pl.multiple_of(q * rows + i * CHUNK, CHUNK), CHUNK)
-            real, imag = t_ref[row, :block], t_ref[row, block:]
+            real, imag = t_ref[q, at, :block], t_ref[q, at, block:]
             if q:
                 cosine, sine = tw_ref[q, 0:1, :], tw_ref[q, 1:2, :]
                 real, imag = real * cosine - imag * sine, imag * cosine + real * sine
@@ -337,22 +340,52 @@
     lax.fori_loop(0, rows // CHUNK, gather, 0)
 
 
-def exchange_kernel(dists, pixes, in_ref, out_ref, send_sem, recv_sem, own_sem):
+def local_copy_spec():
+    return pl.BlockSpec(memory_space=pl.ANY)
+
+
+def remote(src, dst, send_sem, recv_sem, device_id):
+    return pltpu.make_async_remote_copy(
+        src_ref=src,
+        dst_ref=dst,
+        send_sem=send_sem,
+        recv_sem=recv_sem,
+        device_id=device_id,
+        device_id_type=pl.DeviceIdType.MESH,
+    )
+
+
+def gain_factors(defocus, rate, squared):
+    envelope = jnp.exp(-rate * squared)
+    angle = defocus * squared
+    return envelope * jnp.sin(angle), envelope * jnp.cos(angle)
+
+
+def exchange_kernel(
+    dists, pixes, in_ref, own_ref, out_ref, f_ref, g_ref,
+    held, send_sem, recv_sem, own_sem, small_send, small_recv, small_own,
+):
     dist, pix = lax.axis_index("dist"), lax.axis_index("pix")
     count = dists * pixes
     me = dist * pixes + pix
+
+    def small(step, slot):
+        return remote(
+            own_ref, held.at[slot], small_send.at[step], small_recv.at[step], {"dist": (dist + step) % dists}
+        )
+
+    for step in range(1, dists):
+        small(step, dist).start()
+    small_copy = pltpu.make_async_copy(own_ref, held.at[dist], small_own)
+    small_copy.start()
     own = pltpu.make_async_copy(in_ref.at[me], out_ref.at[me], own_sem)
     own.start()
 
     def copy(step):
         target = (me + step) % count
-        return pltpu.make_async_remote_copy(
-            src_ref=in_ref.at[target],
-            dst_ref=out_ref.at[me],
-            send_sem=send_sem.at[step],
-            recv_sem=recv_sem.at[step],
-            device_id={"dist": target // pixes, "pix": target % pixes},
-            device_id_type=pl.DeviceIdType.MESH,
+        return remote(
+            in_ref.at[target], out_ref.at[me], send_sem.at[step], recv_sem.at[step],
+            {"dist": target // pixes, "pix": target % pixes},
         )
 
     def start(step, carry):
@@ -362,103 +395,132 @@
     def finish(step, carry):
         copy(step).wait_send()
         source = (me + count - step) % count
-        pltpu.make_async_remote_copy(
-            src_ref=in_ref.at[source],
-            dst_ref=out_ref.at[source],
-            send_sem=send_sem.at[step],
-            recv_sem=recv_sem.at[step],
-            device_id={"dist": source // pixes, "pix": source % pixes},
-            device_id_type=pl.DeviceIdType.MESH,
+        remote(
+            in_ref.at[source], out_ref.at[source], send_sem.at[step], recv_sem.at[step],
+            {"dist": source // pixes, "pix": source % pixes},
         ).wait_recv()
         return carry
 
     lax.fori_loop(1, count, start, 0)
+
+    for step in range(1, dists):
+        small(step, dist).wait_send()
+        small(step, (dist + dists - step) % dists).wait_recv()
+    small_copy.wait()
+    radix, _, block = f_ref.shape
+    _, width, _ = g_ref.shape
+    row_freq = radix * lax.broadcasted_iota(jnp.int32, (radix, block), 1) + lax.broadcasted_iota(
+        jnp.int32, (radix, block), 0
+    )
+    row_squared = signed_square(row_freq, radix * block)
+    first = me * width
+    col_freq = radix * (first % block + lax.broadcasted_iota(jnp.int32, (width, block), 0)) + first // block
+    col_squared = signed_square(col_freq, radix * block)
+    for d in range(dists):
+        defocus, rate = held[d, 0:1, 0:1], held[d, 1:2, 0:1]
+        sine, cosine = gain_factors(defocus, rate, row_squared)
+        f_ref[:, 2 * d, :] = sine
+        f_ref[:, 2 * d + 1, :] = cosine
+        sine, cosine = gain_factors(defocus, rate, col_squared)
+        g_ref[2 * d] = cosine - ABSORB_RATIO * sine
+        g_ref[2 * d + 1] = sine + ABSORB_RATIO * cosine
+
     lax.fori_loop(1, count, finish, 0)
     own.wait()
 
 
-def exchange(dists, pixes, array):
+def exchange(dists, pixes, array, own):
     count = dists * pixes
+    _, _, width, rows = array.shape
     return pl.pallas_call(
         functools.partial(exchange_kernel, dists, pixes),
-        out_shape=jax.ShapeDtypeStruct(array.shape, array.dtype),
-        in_specs=[pl.BlockSpec(memory_space=pl.ANY)],
-        out_specs=pl.BlockSpec(memory_space=pl.ANY),
+        out_shape=(
+            jax.ShapeDtypeStruct(array.shape, array.dtype),
+            jax.ShapeDtypeStruct((RADIX, 2 * dists, rows), jnp.float32),
+            jax.ShapeDtypeStruct((2 * dists, width, rows), jnp.float32),
+        ),
+        in_specs=[local_copy_spec(), pl.BlockSpec(memory_space=pltpu.VMEM)],
+        out_specs=(local_copy_spec(),) + (pl.BlockSpec(memory_space=pltpu.VMEM),) * 2,
         scratch_shapes=[
+            pltpu.VMEM((dists,) + own.shape, jnp.float32),
             pltpu.SemaphoreType.DMA((count,)),
             pltpu.SemaphoreType.DMA((count,)),
+            pltpu.SemaphoreType.DMA,
+            pltpu.SemaphoreType.DMA((dists,)),
+            pltpu.SemaphoreType.DMA((dists,)),
+            pltpu.SemaphoreType.DMA,
+        ],
+        compiler_params=pltpu.CompilerParams(has_side_effects=True),
+    )(array, own)
+
+
+RELAY_LAG = 1
+
+
+def relay_kernel(pixes, in_ref, out_ref, send_sem, recv_sem, hop_send, hop_recv, own_sem):
+    dist, pix = lax.axis_index("dist"), lax.axis_index("pix")
+    mate = dist + 1 - 2 * (dist % 2)
+    across = (dist + 2) % 4
+    corner = (mate + 2) % 4
+
+    def first(step, source):
+        target = (pix + step) % pixes
+        return remote(
+            in_ref.at[target], out_ref.at[dist, source], send_sem.at[step], recv_sem.at[step], {"pix": target}
+        )
+
+    def source_of(step):
+        return (pix + pixes - step) % pixes
+
+    def hop(owner, step, kind, target):
+        block = out_ref.at[owner, source_of(step)]
+        return remote(block, block, hop_send.at[kind, step], hop_recv.at[kind, step], {"dist": target})
+
+    own = pltpu.make_async_copy(in_ref.at[pix], out_ref.at[dist, pix], own_sem)
+    own.start()
+    for step in range(1, pixes):
+        first(step, pix).start()
+
+    def relay(step):
+        hop(across, step, 0, across).wait_recv()
+        hop(across, step, 2, mate).start()
+
+    for step in range(pixes):
+        if step == 0:
+            own.wait()
+        else:
+            first(step, source_of(step)).wait_recv()
+        hop(dist, step, 0, across).start()
+        hop(dist, step, 1, mate).start()
+        if step >= RELAY_LAG:
+            relay(step - RELAY_LAG)
+    for step in range(pixes - RELAY_LAG, pixes):
+        relay(step)
+    for step in range(pixes):
+        if step:
+            first(step, pix).wait_send()
+        hop(dist, step, 0, across).wait_send()
+        hop(dist, step, 1, mate).wait_send()
+        hop(mate, step, 1, mate).wait_recv()
+        hop(across, step, 2, mate).wait_send()
+        hop(corner, step, 2, mate).wait_recv()
+
+
+def relay_all(dists, pixes, array):
+    return pl.pallas_call(
+        functools.partial(relay_kernel, pixes),
+        out_shape=jax.ShapeDtypeStruct((dists,) + array.shape, array.dtype),
+        in_specs=[local_copy_spec()],
+        out_specs=local_copy_spec(),
+        scratch_shapes=[
+            pltpu.SemaphoreType.DMA((pixes,)),
+            pltpu.SemaphoreType.DMA((pixes,)),
+            pltpu.SemaphoreType.DMA((3, pixes)),
+            pltpu.SemaphoreType.DMA((3, pixes)),
             pltpu.SemaphoreType.DMA,
         ],
         compiler_params=pltpu.CompilerParams(has_side_effects=True),
     )(array)
-
-
-GATHER_PIECES = 4
-
-
-def gather_kernel(in_ref, out_ref, sems, own_sem):
-    dist = lax.axis_index("dist")
-    rows = in_ref.shape[1]
-    piece = rows // GATHER_PIECES
-    mate = dist + 1 - 2 * (dist % 2)
-    across = (dist + 2) % 4
-    corner = (mate + 2) % 4
-
-    def at(owner, c):
-        return out_ref.at[:, pl.ds(pl.multiple_of(owner * rows + c * piece, piece), piece), :]
-
-    def send(src, owner, c, kind, target):
-        return pltpu.make_async_remote_copy(
-            src_ref=src,
-            dst_ref=at(owner, c),
-            send_sem=sems.at[0, kind, c],
-            recv_sem=sems.at[1, kind, c],
-            device_id={"dist": target},
-            device_id_type=pl.DeviceIdType.MESH,
-        )
-
-    def local(c):
-        return in_ref.at[:, pl.ds(c * piece, piece), :]
-
-    own = pltpu.make_async_copy(in_ref, out_ref.at[:, pl.ds(pl.multiple_of(dist * rows, rows), rows), :], own_sem)
-    for c in range(GATHER_PIECES):
-        send(local(c), dist, c, 0, across).start()
-    for c in range(GATHER_PIECES):
-        send(local(c), dist, c, 1, mate).start()
-    own.start()
-    for c in range(GATHER_PIECES):
-        send(local(c), across, c, 0, across).wait_recv()
-        send(at(across, c), across, c, 2, mate).start()
-    for c in range(GATHER_PIECES):
-        send(local(c), dist, c, 0, across).wait_send()
-        send(local(c), mate, c, 1, mate).wait()
-        send(at(across, c), across, c, 2, mate).wait_send()
-        send(at(across, c), corner, c, 2, mate).wait_recv()
-    own.wait()
-
-
-def gather_dist(dists, array):
-    pair, rows, columns = array.shape
-    return pl.pallas_call(
-        gather_kernel,
-        out_shape=jax.ShapeDtypeStruct((pair, dists * rows, columns), array.dtype),
-        in_specs=[pl.BlockSpec(memory_space=pl.ANY)],
-        out_specs=pl.BlockSpec(memory_space=pl.ANY),
-        scratch_shapes=[pltpu.SemaphoreType.DMA((2, 3, GATHER_PIECES)), pltpu.SemaphoreType.DMA],
-        compiler_params=pltpu.CompilerParams(has_side_effects=True),
-    )(array)
-
-
-def freq_square(order, period):
-    freq = RADIX * (order % (period // RADIX)) + order // (period // RADIX)
-    return signed_square(freq, period)
-
-
-def gain_factors(defocus, blurring, squared):
-    envelope = jnp.exp(-blurring[:, None] * squared)
-    sine = envelope * jnp.sin(defocus[:, None] * squared)
-    cosine = envelope * jnp.cos(defocus[:, None] * squared)
-    return sine, cosine
 
 
 def vmem_call(kernel, out_shape, scratch, *args):
@@ -480,7 +542,6 @@
     width = columns // count
     per_q = block // width
     total_rows = rows * pixes
-    out_rows = rows // dists
 
     turns = np.outer(np.arange(block), np.arange(block)) % block * (2.0 * np.pi / block)
     cosine, sine = np.cos(turns), np.sin(turns)
@@ -494,20 +555,7 @@
     tw = np.stack([np.cos(twist), np.sin(twist)], axis=1).astype(np.float32)
     twc = np.concatenate([np.cos(twist).T, np.sin(twist).T], axis=1).astype(np.float32)
 
-    both = lax.all_gather(jnp.concatenate([defocus, blurring]), "dist")
-    defocus_all, blurring_all = both[:, 0], both[:, 1]
-    row_sine, row_cosine = gain_factors(
-        defocus_all, blurring_all, freq_square(jnp.arange(total_rows, dtype=jnp.int32), total_rows)[None]
-    )
-    me = lax.axis_index("dist") * pixes + lax.axis_index("pix")
-    col_sine, col_cosine = gain_factors(
-        defocus_all, blurring_all, freq_square(me * width + jnp.arange(width, dtype=jnp.int32), columns)[None]
-    )
-    f_table = jnp.stack([row_sine, row_cosine], axis=1).reshape(2 * dists, RADIX, rows).transpose(1, 0, 2)
-    g_table = jnp.stack(
-        [col_cosine - ABSORB_RATIO * col_sine, col_sine + ABSORB_RATIO * col_cosine], axis=1
-    ).reshape(2 * dists, width, 1)
-    g_table = jnp.broadcast_to(g_table, (2 * dists, width, rows))
+    own = jnp.broadcast_to(jnp.concatenate([defocus, blurring] * 4)[:, None], (8, 128))
 
     spectra = vmem_call(
         col_forward_kernel,
@@ -515,7 +563,7 @@
         [pltpu.VMEM((RADIX, rows, 2 * block), jnp.bfloat16)] * 2,
         images, th, tl, tw,
     )
-    received = exchange(dists, pixes, spectra.reshape(count, 2, width, rows))
+    received, f_table, g_table = exchange(dists, pixes, spectra.reshape(count, 2, width, rows), own)
     back = vmem_call(
         functools.partial(middle_kernel, 1.0 / (total_rows * columns)),
         (pixes, rows, 2 * width),
@@ -523,16 +571,14 @@
         + [pltpu.VMEM((RADIX, rows, 2 * width), jnp.float32)],
         received.reshape(dists, pixes, 2, width, rows), th, tl, tw, twc, f_table, g_table,
     )
-    back = back.reshape(pixes, dists, out_rows, 2 * width).transpose(1, 0, 2, 3)
-    arrived = exchange(dists, pixes, back.reshape(count, out_rows, 2 * width))
-    phase = vmem_call(
+    arrived = relay_all(dists, pixes, back)
+    return vmem_call(
         col_inverse_kernel,
-        (2, out_rows, columns),
-        [pltpu.VMEM((RADIX * out_rows, 2 * block), jnp.bfloat16)] * 2
-        + [pltpu.VMEM((RADIX * out_rows, 2 * block), jnp.float32)],
-        arrived.reshape(RADIX, per_q, out_rows, 2 * width), ph, pl_, tw,
-    )
-    return gather_dist(dists, phase)
+        (2, rows, columns),
+        [pltpu.VMEM((rows, 2 * block), jnp.bfloat16)] * 2
+        + [pltpu.VMEM((RADIX, rows, 2 * block), jnp.float32)],
+        arrived.reshape(RADIX, per_q, rows, 2 * width), ph, pl_, tw,
+    )
 
 
 def body(contrast, defocus, blurring):

time: 226 us -> 193 us (0.85)
  Pallas kernels: 208 us -> 189 us
  local copies, waits for them, and re-layouts: 9.38 us -> 0.75 us
  blocking collectives: 5.83 us -> 0 us
    pallas_call x2 -> x1, Pallas kernels: 137 us -> 101 us  [exchange(): pl.pallas_call(functools.partial(exchange_kernel, dists, pixes), out_shap...]
    pallas_call x1, Pallas kernels: 37 us -> 47.1 us  [relay_all(): pl.pallas_call(functools.partial(relay_kernel, pixes), out_shape=jax.Shap...]
    pallas_call x3, Pallas kernels: 34.2 us -> 40.8 us  [vmem_call(): pl.pallas_call(kernel, out_shape=jax.ShapeDtypeStruct(out_shape, jnp.floa...]
    unnamed x1 -> x0, blocking collectives: 5.83 us -> none
    unnamed x5 -> x0, local copies, waits for them, and re-layouts: 5.29 us -> none
    reshape x3 -> x0, local copies, waits for them, and re-layouts: 3.02 us -> none  [the longest x1 2.33 us: fast_body(): back = back.reshape(pixes, dists, out_rows, 2 * width).transpose(1, 0, 2, 3)]
where the time goes in v2:
time: 193 us; the launch traced here: 191 us
  Pallas kernels  189 us (98%)
    pallas_call x1, Pallas kernels, exchange(): pl.pallas_call(functools.partial(exchange_kernel, dists, pixes), out_shap...  101 us
    pallas_call x1, Pallas kernels, relay_all(): pl.pallas_call(functools.partial(relay_kernel, pixes), out_shape=jax.Shap...  47.1 us
    pallas_call x3, Pallas kernels, vmem_call(): pl.pallas_call(kernel, out_shape=jax.ShapeDtypeStruct(out_shape, jnp.floa...  40.8 us

profile of v2, /device:TPU:0, one launch (start us, length us, event | category | flops | bytes accessed | tf_op | source)
XLA Modules:
  0.0 190.8 jit_solution(9493689507982938431)
XLA Ops:
  1.3 0.1 concatenate.3
  1.4 0.7 broadcast_in_dim.2.own_ref
  2.0 10.9 %shard_map.91 = f32[8,4,2,64,256]{4,3,2,1,0:T(8,128)} custom-call(f32[2,256,2048]{2,1,0:T(8,128)} %bitcast.6, bf16[512,512]{1,0:T(8,128)(2,1)} %constant.12.clone.th_ref, bf16[512,512]{1,0:T(8,128)(2,1)} %constant.13.clone.tl_ref, f32[8,2,256]{2,1,0:T(2,128)} %constant.14.clone.tw_ref), custom_call_target="tpu_custom_call" | custom-call | tf_op jit(solution)/shard_map/pallas_call | solution.py:527
  12.9 100.8 %shard_map.92 = (f32[32,2,64,256]{3,2,1,0:T(8,128)}, f32[8,8,256]{2,1,0:T(8,128)}, f32[8,64,256]{2,1,0:T(8,128)}) custom-call(f32[32,2,64,256]{3,2,1,0:T(8,128)} %bitcast.5, f32[8,128]{1,0:T(8,128)} %broadcast_in_dim.2.own_ref), custom_call_target="tpu_custom_call" | custom-call | tf_op jit(solution)/shard_map/pallas_call | solution.py:435
  113.7 19.6 %shard_map.93.in_ref = f32[8,256,128]{2,1,0:T(8,128)} custom-call(f32[4,8,2,64,256]{4,3,2,1,0:T(8,128)} %bitcast.7, bf16[512,512]{1,0:T(8,128)(2,1)} %constant.12.clone.th_ref, bf16[512,512]{1,0:T(8,128)(2,1)} %constant.13.clone.tl_ref, f32[8,2,256]{2,1,0:T(2,128)} %constant.14.clone.tw_ref, f32[256,16]{1,0:T(8,128)} %constant.15.clone.twc_ref, ...), custom_call_target="tpu_custom_call" | custom-call | tf_op jit(solution)/shard_map/pallas_call | solution.py:527
  133.3 47.1 %shard_map.94 = f32[4,8,256,128]{3,2,1,0:T(8,128)} custom-call(f32[8,256,128]{2,1,0:T(8,128)} %shard_map.93.in_ref), custom_call_target="tpu_custom_call" | custom-call | tf_op jit(solution)/shard_map/pallas_call | solution.py:510
  180.4 10.3 %shard_map.95 = f32[2,256,2048]{2,1,0:T(8,128)} custom-call(f32[8,4,256,128]{3,2,1,0:T(8,128)} %bitcast.4, bf16[512,512]{1,0:T(8,128)(2,1)} %constant.16.clone.th_ref, bf16[512,512]{1,0:T(8,128)(2,1)} %constant.17.clone.tl_ref, f32[8,2,256]{2,1,0:T(2,128)} %constant.14.clone.tw_ref), custom_call_target="tpu_custom_call" | custom-call | tf_op jit(solution)/shard_map/pallas_call | solution.py:527

commit v3 on v2

--- a/solution.py
+++ b/solution.py
@@ -196,10 +196,9 @@
 pair_dft = functools.partial(small_dft, turn=pair_turn, add=pair_add, sub=pair_sub)
 
 
-def col_forward_kernel(x_ref, th_ref, tl_ref, tw_ref, out_ref, yh_ref, yl_ref):
+def col_spread(x_ref, tw_ref, yh_ref, yl_ref):
     _, rows, columns = x_ref.shape
     block = columns // RADIX
-    per_q, _, width, _ = out_ref.shape[1:]
 
     def spread(i, carry):
         at = pl.ds(pl.multiple_of(i * CHUNK, CHUNK), CHUNK)
@@ -218,17 +217,6 @@
         return carry
 
     lax.fori_loop(0, rows // CHUNK, spread, 0)
-
-    def transform(q, carry):
-        table = (th_ref[...], tl_ref[...])
-        result = dot3(dot_nt, table, (yh_ref[q], yl_ref[q]))
-        for part in range(per_q):
-            for half in range(2):
-                first = half * block + part * width
-                out_ref[q, part, half] = result[first : first + width]
-        return carry
-
-    lax.fori_loop(0, RADIX, transform, 0)
 
 
 def middle_kernel(scale, in_ref, th_ref, tl_ref, tw_ref, twc_ref, f_ref, g_ref, out_ref, yh_ref, yl_ref, t_ref):
@@ -278,7 +266,7 @@
         t_ref[q] = dot3(dot_nt, upper, split_bf16(stacked))
         return carry
 
-    lax.fori_loop(0, RADIX, transform, 0)
+    lax.fori_loop(0, RADIX, transform, 0, unroll=2)
 
     lane = lax.broadcasted_iota(jnp.int32, (CHUNK, 2 * width), 1)
     flip = jnp.where(lane < width, -1.0, 1.0).astype(jnp.float32)
@@ -362,8 +350,8 @@
 
 
 def exchange_kernel(
-    dists, pixes, in_ref, own_ref, out_ref, f_ref, g_ref,
-    held, send_sem, recv_sem, own_sem, small_send, small_recv, small_own,
+    dists, pixes, x_ref, th_ref, tl_ref, tw_ref, own_ref, out_ref, f_ref, g_ref,
+    yh_ref, yl_ref, in_ref, held, send_sem, recv_sem, own_sem, small_send, small_recv, small_own,
 ):
     dist, pix = lax.axis_index("dist"), lax.axis_index("pix")
     count = dists * pixes
@@ -379,7 +367,6 @@
     small_copy = pltpu.make_async_copy(own_ref, held.at[dist], small_own)
     small_copy.start()
     own = pltpu.make_async_copy(in_ref.at[me], out_ref.at[me], own_sem)
-    own.start()
 
     def copy(step):
         target = (me + step) % count
@@ -388,8 +375,36 @@
             {"dist": target // pixes, "pix": target % pixes},
         )
 
-    def start(step, carry):
-        copy(step).start()
+    block = x_ref.shape[2] // RADIX
+    width = in_ref.shape[2]
+    per_q = block // width
+
+    def send(q):
+        for part in range(per_q):
+            step = (q * per_q + part + count - me) % count
+
+            @pl.when(step != 0)
+            def _():
+                copy(step).start()
+
+    def order(i):
+        return (me // per_q + 1 + i) % RADIX
+
+    col_spread(x_ref, tw_ref, yh_ref, yl_ref)
+
+    def transform(i, carry):
+        q = order(i)
+        table = (th_ref[...], tl_ref[...])
+        result = dot3(dot_nt, table, (yh_ref[q], yl_ref[q]))
+        for part in range(per_q):
+            for half in range(2):
+                first = half * block + part * width
+                in_ref[q * per_q + part, half] = result[first : first + width]
+
+        @pl.when(i > 0)
+        def _():
+            send(order(i + RADIX - 1))
+
         return carry
 
     def finish(step, carry):
@@ -401,14 +416,15 @@
         ).wait_recv()
         return carry
 
-    lax.fori_loop(1, count, start, 0)
+    lax.fori_loop(0, RADIX, transform, 0)
 
     for step in range(1, dists):
         small(step, dist).wait_send()
         small(step, (dist + dists - step) % dists).wait_recv()
     small_copy.wait()
-    radix, _, block = f_ref.shape
-    _, width, _ = g_ref.shape
+    send(order(RADIX - 1))
+    own.start()
+    radix = RADIX
     row_freq = radix * lax.broadcasted_iota(jnp.int32, (radix, block), 1) + lax.broadcasted_iota(
         jnp.int32, (radix, block), 0
     )
@@ -429,19 +445,23 @@
     own.wait()
 
 
-def exchange(dists, pixes, array, own):
+def exchange(dists, pixes, images, th, tl, tw, own):
     count = dists * pixes
-    _, _, width, rows = array.shape
+    _, rows, columns = images.shape
+    width = columns // count
     return pl.pallas_call(
         functools.partial(exchange_kernel, dists, pixes),
         out_shape=(
-            jax.ShapeDtypeStruct(array.shape, array.dtype),
+            jax.ShapeDtypeStruct((count, 2, width, rows), jnp.float32),
             jax.ShapeDtypeStruct((RADIX, 2 * dists, rows), jnp.float32),
             jax.ShapeDtypeStruct((2 * dists, width, rows), jnp.float32),
         ),
-        in_specs=[local_copy_spec(), pl.BlockSpec(memory_space=pltpu.VMEM)],
+        in_specs=[pl.BlockSpec(memory_space=pltpu.VMEM)] * 5,
         out_specs=(local_copy_spec(),) + (pl.BlockSpec(memory_space=pltpu.VMEM),) * 2,
         scratch_shapes=[
+            pltpu.VMEM((RADIX, rows, 2 * columns // RADIX), jnp.bfloat16),
+            pltpu.VMEM((RADIX, rows, 2 * columns // RADIX), jnp.bfloat16),
+            pltpu.VMEM((count, 2, width, rows), jnp.float32),
             pltpu.VMEM((dists,) + own.shape, jnp.float32),
             pltpu.SemaphoreType.DMA((count,)),
             pltpu.SemaphoreType.DMA((count,)),
@@ -451,7 +471,7 @@
             pltpu.SemaphoreType.DMA,
         ],
         compiler_params=pltpu.CompilerParams(has_side_effects=True),
-    )(array, own)
+    )(images, th, tl, tw, own)
 
 
 RELAY_LAG = 1
@@ -474,7 +494,8 @@
 
     def hop(owner, step, kind, target):
         block = out_ref.at[owner, source_of(step)]
-        return remote(block, block, hop_send.at[kind, step], hop_recv.at[kind, step], {"dist": target})
+        begin = in_ref.at[pix] if step == 0 and kind < 2 else block
+        return remote(begin, block, hop_send.at[kind, step], hop_recv.at[kind, step], {"dist": target})
 
     own = pltpu.make_async_copy(in_ref.at[pix], out_ref.at[dist, pix], own_sem)
     own.start()
@@ -486,9 +507,7 @@
         hop(across, step, 2, mate).start()
 
     for step in range(pixes):
-        if step == 0:
-            own.wait()
-        else:
+        if step:
             first(step, source_of(step)).wait_recv()
         hop(dist, step, 0, across).start()
         hop(dist, step, 1, mate).start()
@@ -496,6 +515,7 @@
             relay(step - RELAY_LAG)
     for step in range(pixes - RELAY_LAG, pixes):
         relay(step)
+    own.wait()
     for step in range(pixes):
         if step:
             first(step, pix).wait_send()
@@ -557,13 +577,7 @@
 
     own = jnp.broadcast_to(jnp.concatenate([defocus, blurring] * 4)[:, None], (8, 128))
 
-    spectra = vmem_call(
-        col_forward_kernel,
-        (RADIX, per_q, 2, width, rows),
-        [pltpu.VMEM((RADIX, rows, 2 * block), jnp.bfloat16)] * 2,
-        images, th, tl, tw,
-    )
-    received, f_table, g_table = exchange(dists, pixes, spectra.reshape(count, 2, width, rows), own)
+    received, f_table, g_table = exchange(dists, pixes, images, th, tl, tw, own)
     back = vmem_call(
         functools.partial(middle_kernel, 1.0 / (total_rows * columns)),
         (pixes, rows, 2 * width),

time: 193 us -> 187 us (0.969)
  Pallas kernels: 189 us -> 182 us
    pallas_call x3 -> x2, Pallas kernels: 40.8 us -> 27.2 us  [vmem_call(): pl.pallas_call(kernel, out_shape=jax.ShapeDtypeStruct(out_shape, jnp.floa...]
    pallas_call x1, Pallas kernels: 101 us -> 109 us  [exchange(): pl.pallas_call(functools.partial(exchange_kernel, dists, pixes), out_shap...]
where the time goes in v3:
time: 187 us; the launch traced here: 184 us
  Pallas kernels  182 us (97%)
    pallas_call x1, Pallas kernels, exchange(): pl.pallas_call(functools.partial(exchange_kernel, dists, pixes), out_shap...  109 us
    pallas_call x1, Pallas kernels, relay_all(): pl.pallas_call(functools.partial(relay_kernel, pixes), out_shape=jax.Shap...  46.5 us
    pallas_call x2, Pallas kernels, vmem_call(): pl.pallas_call(kernel, out_shape=jax.ShapeDtypeStruct(out_shape, jnp.floa...  27.2 us

profile of v3, /device:TPU:0, one launch (start us, length us, event | category | flops | bytes accessed | tf_op | source)
XLA Modules:
  0.0 184.3 jit_solution(6295732471982164799)
XLA Ops:
  1.3 0.1 concatenate.3
  1.4 0.7 broadcast_in_dim.2.own_ref
  2.1 108.6 %shard_map.91 = (f32[32,2,64,256]{3,2,1,0:T(8,128)}, f32[8,8,256]{2,1,0:T(8,128)}, f32[8,64,256]{2,1,0:T(8,128)}) custom-call(f32[2,256,2048]{2,1,0:T(8,128)} %bitcast.4, bf16[512,512]{1,0:T(8,128)(2,1)} %constant.12.clone.th_ref, bf16[512,512]{1,0:T(8,128)(2,1)} %constant.13.clone.tl_ref, f32[8,2,256]{2,1,0:T(2,128)} %constant.14.clone.tw_ref, ...), custom_call_target="tpu_custom_call" | custom-call | tf_op jit(solution)/shard_map/pallas_call | solution.py:452
  110.7 16.8 %shard_map.92.in_ref = f32[8,256,128]{2,1,0:T(8,128)} custom-call(f32[4,8,2,64,256]{4,3,2,1,0:T(8,128)} %bitcast.5, bf16[512,512]{1,0:T(8,128)(2,1)} %constant.12.clone.th_ref, bf16[512,512]{1,0:T(8,128)(2,1)} %constant.13.clone.tl_ref, f32[8,2,256]{2,1,0:T(2,128)} %constant.14.clone.tw_ref, f32[256,16]{1,0:T(8,128)} %constant.15.clone.twc_ref, ...), custom_call_target="tpu_custom_call" | custom-call | tf_op jit(solution)/shard_map/pallas_call | solution.py:547
  127.5 46.5 %shard_map.93 = f32[4,8,256,128]{3,2,1,0:T(8,128)} custom-call(f32[8,256,128]{2,1,0:T(8,128)} %shard_map.92.in_ref), custom_call_target="tpu_custom_call" | custom-call | tf_op jit(solution)/shard_map/pallas_call | solution.py:530
  174.0 10.3 %shard_map.94 = f32[2,256,2048]{2,1,0:T(8,128)} custom-call(f32[8,4,256,128]{3,2,1,0:T(8,128)} %bitcast.3, bf16[512,512]{1,0:T(8,128)(2,1)} %constant.16.clone.th_ref, bf16[512,512]{1,0:T(8,128)(2,1)} %constant.17.clone.tl_ref, f32[8,2,256]{2,1,0:T(2,128)} %constant.14.clone.tw_ref), custom_call_target="tpu_custom_call" | custom-call | tf_op jit(solution)/shard_map/pallas_call | solution.py:547
